TPU v7x, 512 devices: a whole 4x8x8 slice. The times are simulated.
512 devices in a mesh: rows: 32 (over y_hi, z), feat: 16 (over y_lo, x, core).
Axes of the slice: x: 4, y: 8 (y_hi: 4, y_lo: 2; y = y_hi * 2 + y_lo), z: 8, core: 2. Of those that a mesh axis runs over, the one named last changes fastest.
Arguments:
- acts: bfloat16 [32768, 8192], P('rows', 'feat'), may hold values from -6 to 6
- out_grads: bfloat16 [32768, 8192], P('rows', 'feat'), may hold values from -6 to 6
- proj_in: bfloat16 [8192, 256], P('feat'), may hold values from -0.0625 to 0.0625
- proj_out: bfloat16 [8192, 256], P('feat'), may hold values from -0.0625 to 0.0625
- assignment: int32 [32768], P('rows'), may hold values from 0 to 255
- codes: int32 [4096, 65536], P('rows', 'feat'), may hold values from -128 to 127
- zero_points: int32 [65536], P('feat'), may hold values from -64 to 63
- scales: float32 [65536], P('feat'), may hold values from 2e-06 to 2e-05
Outputs:
- scores: float32 [256, 4096], P('feat', 'rows')
All inputs are finite; a program needn't handle non-finite values.
Results may differ from a plain program's by a relative error of at most 0.005.
Values may be sent and summed in bfloat16 or wider, within the bound.
No kernel may reach another device: no remote copies, remote signals or barrier semaphores. Data moves between devices by JAX's collectives and lax.ppermute only.
A program may use at most 64 MiB of HBM per device.

v0:
```python
import jax
import jax.numpy as jnp
from jax import lax
from jax.experimental import pallas as pl
from jax.experimental.pallas import tpu as pltpu
from jax.sharding import Mesh
from jax.sharding import PartitionSpec as P


RANK = 256
QUERIES = 256
AXES = ("yh", "zh", "zl", "yl", "x", "c")
ROWS = ("yh", "zh", "zl")
FEAT = ("yl", "x", "c")
NY = 4
NZ = 8
ZH = 2
ZL = 4
NW = 8
NF = 16
NI = 16
NJ = 16
HALF = NI * NJ
LANES = 128
OWNER_ROW = 128
PACKED_ROWS = 144
LINK_GAIN = 256.0
f32 = jnp.float32
bf16 = jnp.bfloat16
f16 = jnp.float16
VMEM = pl.BlockSpec(memory_space=pltpu.VMEM)
SMEM = pl.BlockSpec(memory_space=pltpu.SMEM)
SMALL = pltpu.CompilerParams(vmem_limit_bytes=16 * 2**20)


def exchange(blocks, axes):
    return lax.all_to_all(blocks, axes, 0, 0, tiled=True)


def store_kernel(place_ref, codes_ref, zero_ref, *refs):
    outs, turned = refs[:ZL], refs[ZL]
    zl, c = place_ref[0], place_ref[1]
    for i in range(codes_ref.shape[1] // RANK):
        cols = slice(i * RANK, (i + 1) * RANK)
        turned[...] = (codes_ref[:, cols] - zero_ref[:, cols]).astype(f32).T
        for k in range(ZL):
            for s in range(2):
                for h in range(ZH):
                    block = (h * ZL + (zl ^ k)) * 2 + (c ^ s)
                    rows = pl.ds(pl.multiple_of(block * NJ, NJ), NJ)
                    outs[k][s, h, i * NJ : (i + 1) * NJ, :] = turned[rows, :].astype(bf16)


def store_levels(place, codes, zero_points):
    rows = codes.shape[0]
    step = 4
    return pl.pallas_call(
        store_kernel,
        grid=(NI // step,),
        in_specs=[
            SMEM,
            pl.BlockSpec((rows, step * RANK), lambda g: (0, g)),
            pl.BlockSpec((1, step * RANK), lambda g: (0, g)),
        ],
        out_specs=[pl.BlockSpec((2, ZH, step * NJ, rows), lambda g: (0, 0, g, 0))] * ZL,
        out_shape=[jax.ShapeDtypeStruct((2, ZH, HALF, rows), bf16)] * ZL,
        scratch_shapes=[pltpu.VMEM((RANK, rows), f32)],
        compiler_params=SMALL,
        name="store_levels",
    )(place, codes, zero_points.reshape(1, -1))


def pick_kernel(place_ref, scales_ref, own_ref, other_ref):
    c, z = place_ref[1], place_ref[2]
    own_ref[...] = scales_ref[:, pl.ds(z * 2 + c, 1), :]
    other_ref[...] = scales_ref[:, pl.ds(z * 2 + 1 - c, 1), :]


def pick_scales(place, scales):
    return pl.pallas_call(
        pick_kernel,
        in_specs=[SMEM, VMEM],
        out_specs=[VMEM] * 2,
        out_shape=[jax.ShapeDtypeStruct((NI, 1, NJ), f32)] * 2,
        compiler_params=SMALL,
        name="pick_scales",
    )(place, scales.reshape(NI, NF, NJ))


def pack_kernel(sums_ref, owner_ref, inner_ref, packed_ref):
    values = sums_ref[...] * (1.0 / LINK_GAIN)
    inner_ref[...] = values[:NJ].astype(bf16)
    outer = values[NJ:].astype(bf16)
    owners = owner_ref[...].astype(f32)
    tail = jnp.concatenate([owners, jnp.zeros_like(owners)], axis=0).astype(bf16)
    for r in range(NZ):
        for t in range(NZ):
            packed_ref[r, t * NI : (t + 1) * NI, :] = outer[:, t * LANES : (t + 1) * LANES]
        packed_ref[r, OWNER_ROW:, :] = tail


def pack_tokens(sums, assignment):
    return pl.pallas_call(
        pack_kernel,
        in_specs=[VMEM] * 2,
        out_specs=[VMEM] * 2,
        out_shape=[
            jax.ShapeDtypeStruct((NJ, sums.shape[1]), bf16),
            jax.ShapeDtypeStruct((NZ, PACKED_ROWS, LANES), bf16),
        ],
        compiler_params=SMALL,
        name="pack_tokens",
    )(sums, assignment.reshape(NZ, LANES))


def grads_kernel(inner_ref, own_ref, other_ref, scale_ref, out_ref, acc):
    acc[...] = jnp.zeros_like(acc)
    tiles = 4
    span = tiles * LANES
    query = lax.broadcasted_iota(jnp.int32, (QUERIES, span), 0).astype(f32)

    def row(r, carry):
        owners = own_ref[r, OWNER_ROW:, :].astype(f32)
        for p in range(NZ // tiles):
            inner = inner_ref[r, :, p * span : (p + 1) * span].astype(f32)
            cut = range(p * tiles, (p + 1) * tiles)
            parts = []
            for ref in (own_ref, other_ref):
                outer = jnp.concatenate([ref[r, t * NI : (t + 1) * NI, :] for t in cut], axis=1).astype(f32)
                parts.append((outer[:, None, :] * inner[None, :, :]).reshape(HALF, span).astype(bf16))
            product = jnp.concatenate(parts, axis=0)
            owner = jnp.concatenate([owners[t : t + 1, :] for t in cut], axis=1)
            mine = jnp.where(query == owner, 1.0, 0.0).astype(bf16)
            acc[...] += lax.dot_general(product, mine, (((1,), (1,)), ((), ())), preferred_element_type=f32)
        return carry

    lax.fori_loop(0, NZ, row, 0)
    out_ref[...] = (acc[...].T * scale_ref[...]).astype(bf16)


def query_grads(inner, own, other, scale):
    return pl.pallas_call(
        grads_kernel,
        in_specs=[VMEM] * 4,
        out_specs=VMEM,
        out_shape=jax.ShapeDtypeStruct((QUERIES, 2 * HALF), bf16),
        scratch_shapes=[pltpu.VMEM((2 * HALF, QUERIES), f32)],
        compiler_params=SMALL,
        name="query_grads",
    )(inner, own, other, scale)


def share_kernel(terms_ref, out_ref):
    total = terms_ref[0].astype(f32)
    for y in range(1, NY):
        total += terms_ref[y].astype(f32)
    share = total.astype(bf16)
    for y in range(NY * ZH):
        out_ref[y] = share


def spread_share(terms):
    return pl.pallas_call(
        share_kernel,
        in_specs=[VMEM],
        out_specs=VMEM,
        out_shape=jax.ShapeDtypeStruct((NY * ZH, *terms.shape[1:]), bf16),
        compiler_params=SMALL,
        name="spread_share",
    )(terms)


def terms_kernel(place_ref, scaled_ref, other_ref, *refs):
    own, (keep_ref, send_ref) = refs[:ZL], refs[ZL:]
    zl, c = place_ref[0], place_ref[1]
    for k in range(ZL):
        terms = jnp.zeros((QUERIES, other_ref.shape[3]), f32)
        for h in range(ZH):
            terms += jnp.dot(scaled_ref[h, :, :HALF], own[k][0, h], preferred_element_type=f32)
            terms += jnp.dot(scaled_ref[h, :, HALF:], other_ref[k, h], preferred_element_type=f32)
        terms = terms.reshape(NW, 2, QUERIES // NF, terms.shape[1])
        first, second = terms[:, 0], terms[:, 1]
        keep_ref[zl ^ k] = jnp.where(c == 0, first, second)
        send_ref[zl ^ k] = jnp.where(c == 0, second, first)


def score_terms(place, scaled, own, other):
    shape = jax.ShapeDtypeStruct((ZL, NW, QUERIES // NF, other.shape[3]), f32)
    return pl.pallas_call(
        terms_kernel,
        in_specs=[SMEM] + [VMEM] * (2 + ZL),
        out_specs=[VMEM] * 2,
        out_shape=[shape, shape],
        compiler_params=SMALL,
        name="score_terms",
    )(place, scaled, other, *own)


def local(acts, out_grads, proj_in, proj_out, assignment, codes, zero_points, scales):
    tokens = acts.shape[0]
    zl = lax.axis_index("zl")
    z = lax.axis_index("zh") * ZL + zl
    c = lax.axis_index("c")
    place = jnp.stack([zl, c, z]).astype(jnp.int32)
    flip = [(0, 1), (1, 0)]

    dims = (((0,), (1,)), ((), ()))
    part_inner = lax.dot_general(proj_in, acts, dims, preferred_element_type=f32) * LINK_GAIN
    part_outer = lax.dot_general(proj_out, out_grads, dims, preferred_element_type=f32) * LINK_GAIN
    part_inner = part_inner.astype(f16).reshape(NF, NJ, tokens)
    part_outer = part_outer.astype(f16).reshape(NF, NI, tokens)
    parts = exchange(jnp.concatenate([part_inner, part_outer], axis=1), FEAT)
    sums = jnp.sum(parts.astype(f32), axis=0)

    inner, packed = pack_tokens(sums, assignment)
    own = exchange(packed, ("zh", "zl"))
    swap = [(r * NW + w, w * NW + r) for r in range(NZ) for w in range(NW)]
    inner_swapped = lax.ppermute(inner, ("zh", "zl", "yl", "x"), swap)
    inner_all = exchange(jnp.broadcast_to(inner_swapped[None], (NW, *inner.shape)), ("yl", "x"))
    other = lax.ppermute(own, "c", flip)

    store = list(store_levels(place, codes, zero_points))
    for k in range(1, ZL):
        store[k] = lax.ppermute(store[k], "zl", [(r, r ^ k) for r in range(ZL)])
    store_other = lax.ppermute(jnp.stack([block[1] for block in store]), "c", flip)

    own_scale, other_scale = pick_scales(place, scales)
    other_scale = lax.ppermute(other_scale, "c", flip)
    scale = jnp.concatenate([own_scale, other_scale], axis=0).reshape(1, 2 * HALF)

    grads = query_grads(inner_all, own, other, scale)
    grads = exchange(grads.reshape(NY, QUERIES // NY, 2 * HALF), "yh")
    scaled = exchange(spread_share(grads), ("zh", "yh")).reshape(ZH, QUERIES, 2 * HALF)

    keep, send = score_terms(place, scaled, store, store_other)
    got = lax.ppermute(send, "c", flip)
    terms = (keep + got).astype(bf16).reshape(ZL * NW, QUERIES // NF, codes.shape[0])
    terms = exchange(terms, ("zl", "yl", "x"))
    return jnp.sum(terms.astype(f32), axis=0)


def solution(mesh):
    split = Mesh(mesh.devices.reshape(4, 2, 4, 2, 4, 2), AXES)
    in_specs = (
        P(ROWS, FEAT),
        P(ROWS, FEAT),
        P(FEAT, None),
        P(FEAT, None),
        P(ROWS),
        P(ROWS, FEAT),
        P(FEAT),
        P(FEAT),
    )
    out_specs = P(FEAT, ROWS)
    return jax.shard_map(local, mesh=split, in_specs=in_specs, out_specs=out_specs, check_vma=False)
```

profile of v0, /device:TPU:1, one launch (start us, length us, event | category | flops | bytes accessed | tf_op | source)
XLA Modules:
  0.0 155.4 jit_solution(9649202082284808868)
XLA Ops:
  0.0 1.2 copy-done
  1.2 1.4 fusion
  2.7 1.8 %fusion.1 = f16[256,1024]{1,0:T(8,128)(2,1)S(1)} fusion(bf16[512,256]{1,0:T(8,128)(2,1)} %param.11, bf16[1024,512]{1,0:T(8,128)(2,1)} %param.9), kind=kOutput, calls=%fused_computation.4 | convolution fusion | flops 268959744 | bytes 1835008 | tf_op jit(solution)/shard_map/dot_general | solution.py:209
  4.8 24.7 %all_to_all.30 = f16[16,32,1024]{2,1,0:T(8,128)(2,1)S(1)} all-to-all(f16[16,32,1024]{2,1,0:T(8,128)(2,1)S(1)} %pad_maximum_fusion), channel_id=1, replica_groups=mesh['yh'=4,'zh'=2,'zl'=4,'yl'=2,'x'=4,'c'=2] {'yl','x','c'}, dimensions={0} | all-to-all | bytes 2097152 | tf_op jit(solution)/shard_map/all_to_all | solution.py:37
  29.7 0.7 pack_tokens.1
  30.4 7.3 %all-to-all-start.2 = ((bf16[8,144,128]{2,1,0:T(8,128)(2,1)}), bf16[8,144,128]{2,1,0:T(8,128)(2,1)S(1)}, u32[]{:S(2)}, u32[]{:S(2)}) async-start(bf16[8,144,128]{2,1,0:T(8,128)(2,1)} %get-tuple-element.16), calls=%async_computation.2 | async-start | bytes 589824 | tf_op jit(solution)/shard_map/all_to_all | solution.py:37
  37.7 0.7 collective-permute-start
  38.3 10.0 %all-to-all-done.2.own_ref = bf16[8,144,128]{2,1,0:T(8,128)(2,1)S(1)} async-done(((bf16[8,144,128]{2,1,0:T(8,128)(2,1)}), bf16[8,144,128]{2,1,0:T(8,128)(2,1)S(1)}, u32[]{:S(2)}, u32[]{:S(2)}) %all-to-all-start.2) | async-done | bytes 294944 | tf_op jit(solution)/shard_map/all_to_all | solution.py:37
  48.4 0.7 broadcast_in_dim.2
  49.1 5.9 %all-to-all-start.1 = ((bf16[8,16,1024]{2,1,0:T(8,128)(2,1)}), bf16[8,16,1024]{2,1,0:T(8,128)(2,1)S(1)}, u32[]{:S(2)}, u32[]{:S(2)}) async-start(bf16[8,16,1024]{2,1,0:T(8,128)(2,1)} %broadcast_in_dim.2), calls=%async_computation.1 | async-start | bytes 524288 | tf_op jit(solution)/shard_map/all_to_all | solution.py:37
  55.0 2.8 %collective-permute-start.1 = (bf16[8,144,128]{2,1,0:T(8,128)(2,1)S(1)}, bf16[8,144,128]{2,1,0:T(8,128)(2,1)S(1)}, u32[]{:S(2)}, u32[]{:S(2)}) collective-permute-start(bf16[8,144,128]{2,1,0:T(8,128)(2,1)S(1)} %all-to-all-done.2.own_ref), channel_id=1, source_target_pairs={{0,1},{1,0},{2,3},{3,2},{4,5},{5,4},{6,7},{7,6},{8,9},{9,8},{10,11... | collective-permute-start | bytes 884744 | tf_op jit(solution)/shard_map/ppermute | solution.py:220
  58.0 0.6 pick_scales.1
  58.6 1.9 %collective-permute-start.2 = (f32[16,1,16]{2,1,0:T(1,128)S(1)}, f32[16,1,16]{2,1,0:T(1,128)S(1)}, u32[]{:S(2)}, u32[]{:S(2)}) collective-permute-start(f32[16,1,16]{2,1,0:T(1,128)S(1)} %get-tuple-element.18), channel_id=1, source_target_pairs={{0,1},{1,0},{2,3},{3,2},{4,5},{5,4},{6,7},{7,6},{8,9},{9,8},{10,11... | collective-permute-start | bytes 3080 | tf_op jit(solution)/shard_map/ppermute | solution.py:228
  60.5 1.1 collective-permute-done.2
  61.8 4.1 %query_grads.1 = bf16[256,512]{1,0:T(8,128)(2,1)S(1)} custom-call(bf16[8,16,1024]{2,1,0:T(8,128)(2,1)S(1)} %all-to-all-done.1.inner_ref, bf16[8,144,128]{2,1,0:T(8,128)(2,1)S(1)} %all-to-all-done.2.own_ref, bf16[8,144,128]{2,1,0:T(8,128)(2,1)S(1)} %collective-permute-done.1.other_ref, f32[1,512]{1,0:T(1,128)S(1)} %reshape.32.scale_ref), custom_call_target="tpu_custom_call" | custom-call | tf_op jit(solution)/shard_map/query_grads/pallas_call | solution.py:142
  66.0 14.4 %all_to_all.31.terms_ref = bf16[4,64,512]{2,1,0:T(8,128)(2,1)S(1)} all-to-all(bf16[4,64,512]{2,1,0:T(8,128)(2,1)S(1)} %bitcast.15), channel_id=1, replica_groups=mesh['yh'=4,'zh'=2,'zl'=4,'yl'=2,'x'=4,'c'=2] {'yh'}, dimensions={0} | all-to-all | bytes 524288 | tf_op jit(solution)/shard_map/all_to_all | solution.py:37
  80.4 0.8 spread_share.1
  81.2 8.0 %all-to-all-start.4 = ((bf16[8,64,512]{2,1,0:T(8,128)(2,1)}), bf16[8,64,512]{2,1,0:T(8,128)(2,1)S(1)}, u32[]{:S(2)}, u32[]{:S(2)}) async-start(bf16[8,64,512]{2,1,0:T(8,128)(2,1)} %spread_share.1), calls=%async_computation.4 | async-start | bytes 1048576 | tf_op jit(solution)/shard_map/all_to_all | solution.py:37
  89.3 1.6 %copy-done.1 = s32[128,4096]{1,0:T(8,128)S(1)} copy-done((s32[128,4096]{1,0:T(8,128)S(1)}, s32[128,4096]{1,0:T(8,128)}, u32[]{:S(2)}) %copy-start.1) | copy-done | bytes 2097176
  90.9 1.7 %store_levels.1 = (bf16[2,2,256,128]{3,2,1,0:T(8,128)(2,1)S(1)}, bf16[2,2,256,128]{3,2,1,0:T(8,128)(2,1)S(1)}, bf16[2,2,256,128]{3,2,1,0:T(8,128)(2,1)S(1)}, bf16[2,2,256,128]{3,2,1,0:T(8,128)(2,1)S(1)}) custom-call(s32[3]{0:T(128)S(1)} %pad_add_fusion.place_ref, s32[128,4096]{1,0:T(8,128)S(1)} %copy-done.1, s32[1,4096]{1,0:T(1,128)S(1)} %bitcast.16), custom_call_target="tpu_custom_call" | custom-call | tf_op jit(solution)/shard_map/store_levels/pallas_call | solution.py:57
  92.6 2.2 %collective-permute-start.3 = (bf16[2,2,256,128]{3,2,1,0:T(8,128)(2,1)S(1)}, bf16[2,2,256,128]{3,2,1,0:T(8,128)(2,1)S(1)}, u32[]{:S(2)}, u32[]{:S(2)}) collective-permute-start(bf16[2,2,256,128]{3,2,1,0:T(8,128)(2,1)S(1)} %get-tuple-element.20), channel_id=1, source_target_pairs={{0,16},{16,0},{32,48},{48,32},{1,17},{17,1},{33,49},{49,33},{2,18}... | collective-permute-start | bytes 786440 | tf_op jit(solution)/shard_map/ppermute | solution.py:224
  94.8 2.6 %collective-permute-start.4 = (bf16[2,2,256,128]{3,2,1,0:T(8,128)(2,1)S(1)}, bf16[2,2,256,128]{3,2,1,0:T(8,128)(2,1)S(1)}, u32[]{:S(2)}, u32[]{:S(2)}) collective-permute-start(bf16[2,2,256,128]{3,2,1,0:T(8,128)(2,1)S(1)} %get-tuple-element.21), channel_id=1, source_target_pairs={{0,32},{16,48},{32,0},{48,16},{1,33},{17,49},{33,1},{49,17},{2,34}... | collective-permute-start | bytes 786440 | tf_op jit(solution)/shard_map/ppermute | solution.py:224
  97.4 4.5 %collective-permute-start.5 = (bf16[2,2,256,128]{3,2,1,0:T(8,128)(2,1)S(1)}, bf16[2,2,256,128]{3,2,1,0:T(8,128)(2,1)S(1)}, u32[]{:S(2)}, u32[]{:S(2)}) collective-permute-start(bf16[2,2,256,128]{3,2,1,0:T(8,128)(2,1)S(1)} %get-tuple-element.22), channel_id=1, source_target_pairs={{0,48},{16,32},{32,16},{48,0},{1,49},{17,33},{33,17},{49,1},{2,50}... | collective-permute-start | bytes 786440 | tf_op jit(solution)/shard_map/ppermute | solution.py:224
  101.9 13.0 %collective-permute-done.3.refs_1_ = bf16[2,2,256,128]{3,2,1,0:T(8,128)(2,1)S(1)} collective-permute-done((bf16[2,2,256,128]{3,2,1,0:T(8,128)(2,1)S(1)}, bf16[2,2,256,128]{3,2,1,0:T(8,128)(2,1)S(1)}, u32[]{:S(2)}, u32[]{:S(2)}) %collective-permute-start.3) | collective-permute-done | bytes 262176 | tf_op jit(solution)/shard_map/ppermute | solution.py:224
  115.0 7.7 %collective-permute-done.5.refs_3_ = bf16[2,2,256,128]{3,2,1,0:T(8,128)(2,1)S(1)} collective-permute-done((bf16[2,2,256,128]{3,2,1,0:T(8,128)(2,1)S(1)}, bf16[2,2,256,128]{3,2,1,0:T(8,128)(2,1)S(1)}, u32[]{:S(2)}, u32[]{:S(2)}) %collective-permute-start.5) | collective-permute-done | bytes 262176 | tf_op jit(solution)/shard_map/ppermute | solution.py:224
  122.8 3.1 %collective-permute-start.6 = (bf16[4,2,256,128]{3,2,1,0:T(8,128)(2,1)S(1)}, bf16[4,2,256,128]{3,2,1,0:T(8,128)(2,1)S(1)}, u32[]{:S(2)}, u32[]{:S(2)}) collective-permute-start(bf16[4,2,256,128]{3,2,1,0:T(8,128)(2,1)S(1)} %pad_maximum_fusion.1), channel_id=1, source_target_pairs={{0,1},{1,0},{2,3},{3,2},{4,5},{5,4},{6,7},{7,6},{8,9},{9,8},{10,11... | collective-permute-start | bytes 1572872 | tf_op jit(solution)/shard_map/ppermute | solution.py:225
  125.8 1.5 collective-permute-done.6.other_ref
  127.4 1.2 score_terms.1
  128.6 2.3 %collective-permute-start.7 = (f32[4,8,16,128]{3,2,1,0:T(8,128)S(1)}, f32[4,8,16,128]{3,2,1,0:T(8,128)S(1)}, u32[]{:S(2)}, u32[]{:S(2)}) collective-permute-start(f32[4,8,16,128]{3,2,1,0:T(8,128)S(1)} %get-tuple-element.24), channel_id=1, source_target_pairs={{0,1},{1,0},{2,3},{3,2},{4,5},{5,4},{6,7},{7,6},{8,9},{9,8},{10,11... | collective-permute-start | bytes 786440 | tf_op jit(solution)/shard_map/ppermute | solution.py:236
  130.9 1.1 collective-permute-done.7
  132.1 22.7 %all_to_all.32 = bf16[32,16,128]{2,1,0:T(8,128)(2,1)S(1)} all-to-all(bf16[32,16,128]{2,1,0:T(8,128)(2,1)S(1)} %bitcast.20), channel_id=1, replica_groups=mesh['yh'=4,'zh'=2,'zl'=4,'yl'=2,'x'=4,'c'=2] {'zl','yl','x'}, dimensions={0} | all-to-all | bytes 262144 | tf_op jit(solution)/shard_map/all_to_all | solution.py:37
  154.8 0.6 convert_reduce_fusion.1
  (25 shorter events, 1.0 us)
Async XLA Ops:
  0.0 1.2 copy-start
  4.8 24.9 %copy-start.3 = (s32[1024]{0:T(1024)S(1)}, s32[1024]{0:T(1024)}, u32[]{:S(2)}) copy-start(s32[1024]{0:T(1024)} %param.12) | copy-start | bytes 12292
  4.8 53.1 %copy-start.4 = (f32[4096]{0:T(1024)S(1)}, f32[4096]{0:T(1024)}, u32[]{:S(2)}) copy-start(f32[4096]{0:T(1024)} %param.15) | copy-start | bytes 49156
  30.4 18.0 %all-to-all-start.2 = ((bf16[8,144,128]{2,1,0:T(8,128)(2,1)}), bf16[8,144,128]{2,1,0:T(8,128)(2,1)S(1)}, u32[]{:S(2)}, u32[]{:S(2)}) async-start(bf16[8,144,128]{2,1,0:T(8,128)(2,1)} %get-tuple-element.16), calls=%async_computation.2 | async-start | bytes 589824 | tf_op jit(solution)/shard_map/all_to_all | solution.py:37
  37.7 0.7 collective-permute-start
  49.1 40.2 %copy-start.2 = (s32[4096]{0:T(1024)S(1)}, s32[4096]{0:T(1024)}, u32[]{:S(2)}) copy-start(s32[4096]{0:T(1024)} %param.14) | copy-start | bytes 49156
  49.1 12.7 %all-to-all-start.1 = ((bf16[8,16,1024]{2,1,0:T(8,128)(2,1)}), bf16[8,16,1024]{2,1,0:T(8,128)(2,1)S(1)}, u32[]{:S(2)}, u32[]{:S(2)}) async-start(bf16[8,16,1024]{2,1,0:T(8,128)(2,1)} %broadcast_in_dim.2), calls=%async_computation.1 | async-start | bytes 524288 | tf_op jit(solution)/shard_map/all_to_all | solution.py:37
  55.0 6.8 %collective-permute-start.1 = (bf16[8,144,128]{2,1,0:T(8,128)(2,1)S(1)}, bf16[8,144,128]{2,1,0:T(8,128)(2,1)S(1)}, u32[]{:S(2)}, u32[]{:S(2)}) collective-permute-start(bf16[8,144,128]{2,1,0:T(8,128)(2,1)S(1)} %all-to-all-done.2.own_ref), channel_id=1, source_target_pairs={{0,1},{1,0},{2,3},{3,2},{4,5},{5,4},{6,7},{7,6},{8,9},{9,8},{10,11... | collective-permute-start | bytes 884744 | tf_op jit(solution)/shard_map/ppermute | solution.py:220
  58.6 3.1 %collective-permute-start.2 = (f32[16,1,16]{2,1,0:T(1,128)S(1)}, f32[16,1,16]{2,1,0:T(1,128)S(1)}, u32[]{:S(2)}, u32[]{:S(2)}) collective-permute-start(f32[16,1,16]{2,1,0:T(1,128)S(1)} %get-tuple-element.18), channel_id=1, source_target_pairs={{0,1},{1,0},{2,3},{3,2},{4,5},{5,4},{6,7},{7,6},{8,9},{9,8},{10,11... | collective-permute-start | bytes 3080 | tf_op jit(solution)/shard_map/ppermute | solution.py:228
  81.2 46.1 %all-to-all-start.4 = ((bf16[8,64,512]{2,1,0:T(8,128)(2,1)}), bf16[8,64,512]{2,1,0:T(8,128)(2,1)S(1)}, u32[]{:S(2)}, u32[]{:S(2)}) async-start(bf16[8,64,512]{2,1,0:T(8,128)(2,1)} %spread_share.1), calls=%async_computation.4 | async-start | bytes 1048576 | tf_op jit(solution)/shard_map/all_to_all | solution.py:37
  89.3 1.6 %copy-start.1 = (s32[128,4096]{1,0:T(8,128)S(1)}, s32[128,4096]{1,0:T(8,128)}, u32[]{:S(2)}) copy-start(s32[128,4096]{1,0:T(8,128)} %codes_ref.1) | copy-start | bytes 6291460
  92.6 22.3 %collective-permute-start.3 = (bf16[2,2,256,128]{3,2,1,0:T(8,128)(2,1)S(1)}, bf16[2,2,256,128]{3,2,1,0:T(8,128)(2,1)S(1)}, u32[]{:S(2)}, u32[]{:S(2)}) collective-permute-start(bf16[2,2,256,128]{3,2,1,0:T(8,128)(2,1)S(1)} %get-tuple-element.20), channel_id=1, source_target_pairs={{0,16},{16,0},{32,48},{48,32},{1,17},{17,1},{33,49},{49,33},{2,18}... | collective-permute-start | bytes 786440 | tf_op jit(solution)/shard_map/ppermute | solution.py:224
  94.8 20.2 %collective-permute-start.4 = (bf16[2,2,256,128]{3,2,1,0:T(8,128)(2,1)S(1)}, bf16[2,2,256,128]{3,2,1,0:T(8,128)(2,1)S(1)}, u32[]{:S(2)}, u32[]{:S(2)}) collective-permute-start(bf16[2,2,256,128]{3,2,1,0:T(8,128)(2,1)S(1)} %get-tuple-element.21), channel_id=1, source_target_pairs={{0,32},{16,48},{32,0},{48,16},{1,33},{17,49},{33,1},{49,17},{2,34}... | collective-permute-start | bytes 786440 | tf_op jit(solution)/shard_map/ppermute | solution.py:224
  97.4 25.2 %collective-permute-start.5 = (bf16[2,2,256,128]{3,2,1,0:T(8,128)(2,1)S(1)}, bf16[2,2,256,128]{3,2,1,0:T(8,128)(2,1)S(1)}, u32[]{:S(2)}, u32[]{:S(2)}) collective-permute-start(bf16[2,2,256,128]{3,2,1,0:T(8,128)(2,1)S(1)} %get-tuple-element.22), channel_id=1, source_target_pairs={{0,48},{16,32},{32,16},{48,0},{1,49},{17,33},{33,17},{49,1},{2,50}... | collective-permute-start | bytes 786440 | tf_op jit(solution)/shard_map/ppermute | solution.py:224
  122.8 4.6 %collective-permute-start.6 = (bf16[4,2,256,128]{3,2,1,0:T(8,128)(2,1)S(1)}, bf16[4,2,256,128]{3,2,1,0:T(8,128)(2,1)S(1)}, u32[]{:S(2)}, u32[]{:S(2)}) collective-permute-start(bf16[4,2,256,128]{3,2,1,0:T(8,128)(2,1)S(1)} %pad_maximum_fusion.1), channel_id=1, source_target_pairs={{0,1},{1,0},{2,3},{3,2},{4,5},{5,4},{6,7},{7,6},{8,9},{9,8},{10,11... | collective-permute-start | bytes 1572872 | tf_op jit(solution)/shard_map/ppermute | solution.py:225
  128.6 3.4 %collective-permute-start.7 = (f32[4,8,16,128]{3,2,1,0:T(8,128)S(1)}, f32[4,8,16,128]{3,2,1,0:T(8,128)S(1)}, u32[]{:S(2)}, u32[]{:S(2)}) collective-permute-start(f32[4,8,16,128]{3,2,1,0:T(8,128)S(1)} %get-tuple-element.24), channel_id=1, source_target_pairs={{0,1},{1,0},{2,3},{3,2},{4,5},{5,4},{6,7},{7,6},{8,9},{9,8},{10,11... | collective-permute-start | bytes 786440 | tf_op jit(solution)/shard_map/ppermute | solution.py:236
where the time goes:
time: 156 us; the launch traced here: 155 us
  blocking collectives  61.8 us (40%)
  starting transfers between devices  41.3 us (26%)
  waiting for transfers between devices  34.5 us (22%)
  Pallas kernels  9.21 us (6%)
  local copies, waits for them, and re-layouts  3.77 us (2%)
  matrix products  3.24 us (2%)
    all_to_all x3, blocking collectives, exchange(): return lax.all_to_all(blocks, axes, 0, 0, tiled=True)  61.8 us
    all_to_all x3, starting transfers between devices, exchange(): return lax.all_to_all(blocks, axes, 0, 0, tiled=True)  21.2 us
    ppermute x3, waiting for transfers between devices, local(): store[k] = lax.ppermute(store[k], 'zl', [(r, r ^ k) for r in range(ZL)])  20.7 us
    all_to_all x3, waiting for transfers between devices, exchange(): return lax.all_to_all(blocks, axes, 0, 0, tiled=True)  10 us
    ppermute x3, starting transfers between devices, local(): store[k] = lax.ppermute(store[k], 'zl', [(r, r ^ k) for r in range(ZL)])  9.27 us
    pallas_call x1, Pallas kernels, query_grads(): pl.pallas_call(grads_kernel, in_specs=[VMEM] * 4, out_specs=VMEM, out_sha...  4.14 us
  transfers between devices with their start and end apart: 11, of which 6 were waited for; matrix products, arithmetic and copies ran while one was open for 0% of the time, Pallas kernels for 1%

commit v1 on v0

--- a/solution.py
+++ b/solution.py
@@ -9,8 +9,8 @@
 
 RANK = 256
 QUERIES = 256
-AXES = ("yh", "zh", "zl", "yl", "x", "c")
-ROWS = ("yh", "zh", "zl")
+AXES = ("yh", "zl", "zh", "yl", "x", "c")
+ROWS = ("yh", "zl", "zh")
 FEAT = ("yl", "x", "c")
 NY = 4
 NZ = 8
@@ -24,7 +24,7 @@
 LANES = 128
 OWNER_ROW = 128
 PACKED_ROWS = 144
-LINK_GAIN = 256.0
+LINK_GAIN = 128.0
 f32 = jnp.float32
 bf16 = jnp.bfloat16
 f16 = jnp.float16
@@ -46,7 +46,7 @@
         for k in range(ZL):
             for s in range(2):
                 for h in range(ZH):
-                    block = (h * ZL + (zl ^ k)) * 2 + (c ^ s)
+                    block = (c ^ s) * NZ + (zl ^ k) * ZH + h
                     rows = pl.ds(pl.multiple_of(block * NJ, NJ), NJ)
                     outs[k][s, h, i * NJ : (i + 1) * NJ, :] = turned[rows, :].astype(bf16)
 
@@ -72,8 +72,8 @@
 
 def pick_kernel(place_ref, scales_ref, own_ref, other_ref):
     c, z = place_ref[1], place_ref[2]
-    own_ref[...] = scales_ref[:, pl.ds(z * 2 + c, 1), :]
-    other_ref[...] = scales_ref[:, pl.ds(z * 2 + 1 - c, 1), :]
+    own_ref[...] = scales_ref[:, pl.ds(c * NZ + z, 1), :]
+    other_ref[...] = scales_ref[:, pl.ds((1 - c) * NZ + z, 1), :]
 
 
 def pick_scales(place, scales):
@@ -85,6 +85,43 @@
         compiler_params=SMALL,
         name="pick_scales",
     )(place, scales.reshape(NI, NF, NJ))
+
+
+def project_kernel(place_ref, acts_ref, grads_ref, in_ref, out_ref, keep_ref, send_ref, turned, full):
+    c = place_ref[1]
+
+    @pl.when(pl.program_id(0) == 0)
+    def turn():
+        turned[0] = in_ref[...].T
+        turned[1] = out_ref[...].T
+
+    for side, ref in enumerate((acts_ref, grads_ref)):
+        full[side] = lax.dot_general(
+            turned[side], ref[...], (((1,), (1,)), ((), ())), preferred_element_type=f32
+        )
+    for w in range(NW):
+        for ref, core in ((keep_ref, c), (send_ref, 1 - c)):
+            rows = pl.ds(pl.multiple_of((core * NZ + w) * NJ, NJ), NJ)
+            ref[w, :NJ, :] = full[0, rows, :]
+            rows = pl.ds(pl.multiple_of((w * 2 + core) * NI, NI), NI)
+            ref[w, NJ:, :] = full[1, rows, :]
+
+
+def project(place, acts, out_grads, proj_in, proj_out):
+    tokens, depth = acts.shape
+    span = 2 * LANES
+    wide = pl.BlockSpec((span, depth), lambda g: (g, 0))
+    whole = pl.BlockSpec((depth, RANK), lambda g: (0, 0))
+    shape = jax.ShapeDtypeStruct((NW, NJ + NI, tokens), f32)
+    return pl.pallas_call(
+        project_kernel,
+        grid=(tokens // span,),
+        in_specs=[SMEM, wide, wide, whole, whole],
+        out_specs=[pl.BlockSpec((NW, NJ + NI, span), lambda g: (0, 0, g))] * 2,
+        out_shape=[shape] * 2,
+        scratch_shapes=[pltpu.VMEM((2, RANK, depth), bf16), pltpu.VMEM((2, RANK, span), f32)],
+        name="project",
+    )(place, acts, out_grads, proj_in, proj_out)
 
 
 def pack_kernel(sums_ref, owner_ref, inner_ref, packed_ref):
@@ -180,12 +217,12 @@
             terms += jnp.dot(scaled_ref[h, :, HALF:], other_ref[k, h], preferred_element_type=f32)
         terms = terms.reshape(NW, 2, QUERIES // NF, terms.shape[1])
         first, second = terms[:, 0], terms[:, 1]
-        keep_ref[zl ^ k] = jnp.where(c == 0, first, second)
-        send_ref[zl ^ k] = jnp.where(c == 0, second, first)
+        keep_ref[:, zl ^ k] = jnp.where(c == 0, first, second)
+        send_ref[:, zl ^ k] = jnp.where(c == 0, second, first)
 
 
 def score_terms(place, scaled, own, other):
-    shape = jax.ShapeDtypeStruct((ZL, NW, QUERIES // NF, other.shape[3]), f32)
+    shape = jax.ShapeDtypeStruct((NW, ZL, QUERIES // NF, other.shape[3]), f32)
     return pl.pallas_call(
         terms_kernel,
         in_specs=[SMEM] + [VMEM] * (2 + ZL),
@@ -196,27 +233,39 @@
     )(place, scaled, other, *own)
 
 
+def late_kernel(place_ref, out_ref):
+    for i in range(out_ref.shape[0]):
+        out_ref[i] = place_ref[i]
+
+
+def late_place(place):
+    return pl.pallas_call(
+        late_kernel,
+        in_specs=[SMEM],
+        out_specs=SMEM,
+        out_shape=jax.ShapeDtypeStruct(place.shape, place.dtype),
+        name="late_place",
+    )(place)
+
+
 def local(acts, out_grads, proj_in, proj_out, assignment, codes, zero_points, scales):
-    tokens = acts.shape[0]
     zl = lax.axis_index("zl")
-    z = lax.axis_index("zh") * ZL + zl
+    z = zl * ZH + lax.axis_index("zh")
     c = lax.axis_index("c")
     place = jnp.stack([zl, c, z]).astype(jnp.int32)
     flip = [(0, 1), (1, 0)]
 
-    dims = (((0,), (1,)), ((), ()))
-    part_inner = lax.dot_general(proj_in, acts, dims, preferred_element_type=f32) * LINK_GAIN
-    part_outer = lax.dot_general(proj_out, out_grads, dims, preferred_element_type=f32) * LINK_GAIN
-    part_inner = part_inner.astype(f16).reshape(NF, NJ, tokens)
-    part_outer = part_outer.astype(f16).reshape(NF, NI, tokens)
-    parts = exchange(jnp.concatenate([part_inner, part_outer], axis=1), FEAT)
+    keep, send = project(place, acts, out_grads, proj_in, proj_out)
+    got = lax.ppermute(send, "c", flip)
+    parts = ((keep + got) * LINK_GAIN).astype(f16)
+    parts = exchange(parts, ("yl", "x"))
     sums = jnp.sum(parts.astype(f32), axis=0)
 
     inner, packed = pack_tokens(sums, assignment)
-    own = exchange(packed, ("zh", "zl"))
+    own = exchange(packed, ("zl", "zh"))
     swap = [(r * NW + w, w * NW + r) for r in range(NZ) for w in range(NW)]
-    inner_swapped = lax.ppermute(inner, ("zh", "zl", "yl", "x"), swap)
-    inner_all = exchange(jnp.broadcast_to(inner_swapped[None], (NW, *inner.shape)), ("yl", "x"))
+    inner = lax.ppermute(inner, ("zl", "zh", "yl", "x"), swap)
+    inner = exchange(jnp.broadcast_to(inner[None], (NW, *inner.shape)), ("yl", "x"))
     other = lax.ppermute(own, "c", flip)
 
     store = list(store_levels(place, codes, zero_points))
@@ -228,19 +277,20 @@
     other_scale = lax.ppermute(other_scale, "c", flip)
     scale = jnp.concatenate([own_scale, other_scale], axis=0).reshape(1, 2 * HALF)
 
-    grads = query_grads(inner_all, own, other, scale)
+    grads = query_grads(inner, own, other, scale)
     grads = exchange(grads.reshape(NY, QUERIES // NY, 2 * HALF), "yh")
+    place = late_place(place)
     scaled = exchange(spread_share(grads), ("zh", "yh")).reshape(ZH, QUERIES, 2 * HALF)
 
     keep, send = score_terms(place, scaled, store, store_other)
     got = lax.ppermute(send, "c", flip)
-    terms = (keep + got).astype(bf16).reshape(ZL * NW, QUERIES // NF, codes.shape[0])
-    terms = exchange(terms, ("zl", "yl", "x"))
-    return jnp.sum(terms.astype(f32), axis=0)
+    terms = exchange((keep + got).astype(bf16), ("yl", "x"))
+    terms = exchange(jnp.sum(terms.astype(f32), axis=0), "zl")
+    return jnp.sum(terms.reshape(ZL, QUERIES // NF, codes.shape[0]), axis=0)
 
 
 def solution(mesh):
-    split = Mesh(mesh.devices.reshape(4, 2, 4, 2, 4, 2), AXES)
+    split = Mesh(mesh.devices.reshape(4, 4, 2, 2, 4, 2), AXES)
     in_specs = (
         P(ROWS, FEAT),
         P(ROWS, FEAT),

time: 156 us -> 159 us (1.019)
  blocking collectives: 61.8 us -> 48.6 us
  starting transfers between devices: 41.3 us -> 52.9 us
  Pallas kernels: 9.21 us -> 15.2 us
  matrix products: 3.24 us -> 0 us
  local copies, waits for them, and re-layouts: 3.77 us -> 1.62 us
  other arithmetic: 1.35 us -> 2.95 us
    all_to_all x3 -> x4, blocking collectives: 61.8 us -> 48.6 us  [exchange(): return lax.all_to_all(blocks, axes, 0, 0, tiled=True)]
    ppermute x1 -> x2, starting transfers between devices: 2.29 us -> 11 us  [local(): got = lax.ppermute(send, 'c', flip)]
    pallas_call x0 -> x2, Pallas kernels: none -> 6.02 us  [the longest x1 4.84 us: project(): pl.pallas_call(project_kernel, grid=(tokens // span,), in_specs=[SMEM, wi...]
    dot_general x2 -> x0, matrix products: 3.24 us -> none  [the longest x1 1.8 us: local(): lax.dot_general(proj_out, out_grads, dims, preferred_element_type=f32)]
    all_to_all x3, starting transfers between devices: 21.2 us -> 18.6 us  [exchange(): return lax.all_to_all(blocks, axes, 0, 0, tiled=True)]
    ppermute x1 -> x2, waiting for transfers between devices: 1.14 us -> 3.62 us  [local(): got = lax.ppermute(send, 'c', flip)]
    ppermute x1, starting transfers between devices: 2.85 us -> 5.06 us  [local(): other = lax.ppermute(own, 'c', flip)]
    unnamed x10 -> x12, local copies, waits for them, and re-layouts: 2.83 us -> 0.68 us
  transfers between devices with their start and end apart: 11 -> 12, of which waited for: 6 -> 7; matrix products, arithmetic and copies ran while one was open for 0% -> 0% of each run, Pallas kernels for 1% -> 2%
where the time goes in v1:
time: 159 us; the launch traced here: 157 us
  starting transfers between devices  52.9 us (33%)
  blocking collectives  48.6 us (31%)
  waiting for transfers between devices  35.3 us (22%)
  Pallas kernels  15.2 us (10%)
  other arithmetic  2.95 us (2%)
  local copies, waits for them, and re-layouts  1.62 us (1%)
    all_to_all x4, blocking collectives, exchange(): return lax.all_to_all(blocks, axes, 0, 0, tiled=True)  48.6 us
    ppermute x3, waiting for transfers between devices, local(): store[k] = lax.ppermute(store[k], 'zl', [(r, r ^ k) for r in range(ZL)])  20.8 us
    all_to_all x3, starting transfers between devices, exchange(): return lax.all_to_all(blocks, axes, 0, 0, tiled=True)  18.6 us
    ppermute x3, starting transfers between devices, local(): store[k] = lax.ppermute(store[k], 'zl', [(r, r ^ k) for r in range(ZL)])  11.4 us
    ppermute x2, starting transfers between devices, local(): got = lax.ppermute(send, 'c', flip)  11 us
    all_to_all x3, waiting for transfers between devices, exchange(): return lax.all_to_all(blocks, axes, 0, 0, tiled=True)  9.42 us
    ppermute x1, starting transfers between devices, local(): other = lax.ppermute(own, 'c', flip)  5.06 us
    pallas_call x1, Pallas kernels, project(): pl.pallas_call(project_kernel, grid=(tokens // span,), in_specs=[SMEM, wi...  4.84 us
  transfers between devices with their start and end apart: 12, of which 7 were waited for; matrix products, arithmetic and copies ran while one was open for 0% of the time, Pallas kernels for 2%

profile of v1, /device:TPU:1, one launch (start us, length us, event | category | flops | bytes accessed | tf_op | source)
XLA Modules:
  0.0 156.8 jit_solution(8673382074385987014)
XLA Ops:
  0.6 4.8 %project.1 = (f32[8,32,1024]{2,1,0:T(8,128)}, f32[8,32,1024]{2,1,0:T(8,128)}) custom-call(s32[3]{0:T(128)} %pad_add_fusion.place_ref, bf16[1024,512]{1,0:T(8,128)(2,1)} %acts_ref.1, bf16[1024,512]{1,0:T(8,128)(2,1)} %grads_ref.1, bf16[512,256]{1,0:T(8,128)(2,1)} %in_ref.1, bf16[512,256]{1,0:T(8,128)(2,1)} %out_ref.1), custom_call_target="tpu_custom_call" | custom-call | tf_op jit(solution)/shard_map/project/pallas_call | solution.py:116
  5.5 8.7 %collective-permute-start = (f32[8,32,1024]{2,1,0:T(8,128)}, f32[8,32,1024]{2,1,0:T(8,128)S(1)}, u32[]{:S(2)}, u32[]{:S(2)}) collective-permute-start(f32[8,32,1024]{2,1,0:T(8,128)} %get-tuple-element.18), channel_id=1, source_target_pairs={{0,1},{1,0},{2,3},{3,2},{4,5},{5,4},{6,7},{7,6},{8,9},{9,8},{10,11... | collective-permute-start | bytes 3145736 | tf_op jit(solution)/shard_map/ppermute | solution.py:259
  14.2 2.5 %collective-permute-done = f32[8,32,1024]{2,1,0:T(8,128)S(1)} collective-permute-done((f32[8,32,1024]{2,1,0:T(8,128)}, f32[8,32,1024]{2,1,0:T(8,128)S(1)}, u32[]{:S(2)}, u32[]{:S(2)}) %collective-permute-start) | collective-permute-done | bytes 1048608 | tf_op jit(solution)/shard_map/ppermute | solution.py:259
  16.7 1.5 multiply_convert_fusion
  18.2 11.2 %all_to_all.35 = f16[8,32,1024]{2,1,0:T(8,128)(2,1)S(1)} all-to-all(f16[8,32,1024]{2,1,0:T(8,128)(2,1)S(1)} %multiply_convert_fusion), channel_id=1, replica_groups=mesh['yh'=4,'zl'=4,'zh'=2,'yl'=2,'x'=4,'c'=2] {'yl','x'}, dimensions={0} | all-to-all | bytes 1048576 | tf_op jit(solution)/shard_map/all_to_all | solution.py:37
  29.5 0.7 pack_tokens.1
  30.2 7.1 %all-to-all-start.2 = ((bf16[8,144,128]{2,1,0:T(8,128)(2,1)}), bf16[8,144,128]{2,1,0:T(8,128)(2,1)S(1)}, u32[]{:S(2)}, u32[]{:S(2)}) async-start(bf16[8,144,128]{2,1,0:T(8,128)(2,1)} %get-tuple-element.20), calls=%async_computation.2 | async-start | bytes 589824 | tf_op jit(solution)/shard_map/all_to_all | solution.py:37
  37.3 0.7 collective-permute-start.1
  38.0 9.4 %all-to-all-done.2.own_ref = bf16[8,144,128]{2,1,0:T(8,128)(2,1)S(1)} async-done(((bf16[8,144,128]{2,1,0:T(8,128)(2,1)}), bf16[8,144,128]{2,1,0:T(8,128)(2,1)S(1)}, u32[]{:S(2)}, u32[]{:S(2)}) %all-to-all-start.2) | async-done | bytes 294944 | tf_op jit(solution)/shard_map/all_to_all | solution.py:37
  47.4 0.7 broadcast_in_dim.2
  48.1 4.6 %all-to-all-start.1 = ((bf16[8,16,1024]{2,1,0:T(8,128)(2,1)}), bf16[8,16,1024]{2,1,0:T(8,128)(2,1)S(1)}, u32[]{:S(2)}, u32[]{:S(2)}) async-start(bf16[8,16,1024]{2,1,0:T(8,128)(2,1)} %broadcast_in_dim.2), calls=%async_computation.1 | async-start | bytes 524288 | tf_op jit(solution)/shard_map/all_to_all | solution.py:37
  52.8 5.1 %collective-permute-start.2 = (bf16[8,144,128]{2,1,0:T(8,128)(2,1)S(1)}, bf16[8,144,128]{2,1,0:T(8,128)(2,1)S(1)}, u32[]{:S(2)}, u32[]{:S(2)}) collective-permute-start(bf16[8,144,128]{2,1,0:T(8,128)(2,1)S(1)} %all-to-all-done.2.own_ref), channel_id=1, source_target_pairs={{0,1},{1,0},{2,3},{3,2},{4,5},{5,4},{6,7},{7,6},{8,9},{9,8},{10,11... | collective-permute-start | bytes 884744 | tf_op jit(solution)/shard_map/ppermute | solution.py:269
  58.5 1.9 %collective-permute-start.3 = (f32[16,1,16]{2,1,0:T(1,128)S(1)}, f32[16,1,16]{2,1,0:T(1,128)S(1)}, u32[]{:S(2)}, u32[]{:S(2)}) collective-permute-start(f32[16,1,16]{2,1,0:T(1,128)S(1)} %get-tuple-element.22), channel_id=1, source_target_pairs={{0,1},{1,0},{2,3},{3,2},{4,5},{5,4},{6,7},{7,6},{8,9},{9,8},{10,11... | collective-permute-start | bytes 3080 | tf_op jit(solution)/shard_map/ppermute | solution.py:277
  60.4 1.1 collective-permute-done.3
  61.7 4.1 %query_grads.1 = bf16[256,512]{1,0:T(8,128)(2,1)S(1)} custom-call(bf16[8,16,1024]{2,1,0:T(8,128)(2,1)S(1)} %all-to-all-done.1.inner_ref, bf16[8,144,128]{2,1,0:T(8,128)(2,1)S(1)} %all-to-all-done.2.own_ref, bf16[8,144,128]{2,1,0:T(8,128)(2,1)S(1)} %collective-permute-done.2.other_ref, f32[1,512]{1,0:T(1,128)S(1)} %reshape.21.scale_ref), custom_call_target="tpu_custom_call" | custom-call | tf_op jit(solution)/shard_map/query_grads/pallas_call | solution.py:179
  65.9 14.5 %all_to_all.36.terms_ref = bf16[4,64,512]{2,1,0:T(8,128)(2,1)S(1)} all-to-all(bf16[4,64,512]{2,1,0:T(8,128)(2,1)S(1)} %bitcast.8), channel_id=1, replica_groups=mesh['yh'=4,'zl'=4,'zh'=2,'yl'=2,'x'=4,'c'=2] {'yh'}, dimensions={0} | all-to-all | bytes 524288 | tf_op jit(solution)/shard_map/all_to_all | solution.py:37
  80.4 0.8 spread_share.1
  81.2 6.9 %all-to-all-start.4 = ((bf16[8,64,512]{2,1,0:T(8,128)(2,1)}), bf16[8,64,512]{2,1,0:T(8,128)(2,1)S(1)}, u32[]{:S(2)}, u32[]{:S(2)}) async-start(bf16[8,64,512]{2,1,0:T(8,128)(2,1)} %spread_share.1), calls=%async_computation.4 | async-start | bytes 1048576 | tf_op jit(solution)/shard_map/all_to_all | solution.py:37
  88.1 1.7 %store_levels.1 = (bf16[2,2,256,128]{3,2,1,0:T(8,128)(2,1)S(1)}, bf16[2,2,256,128]{3,2,1,0:T(8,128)(2,1)S(1)}, bf16[2,2,256,128]{3,2,1,0:T(8,128)(2,1)S(1)}, bf16[2,2,256,128]{3,2,1,0:T(8,128)(2,1)S(1)}) custom-call(s32[3]{0:T(128)S(1)} %copy-done.2, s32[128,4096]{1,0:T(8,128)S(1)} %copy-done, s32[1,4096]{1,0:T(1,128)S(1)} %bitcast.9), custom_call_target="tpu_custom_call" | custom-call | tf_op jit(solution)/shard_map/store_levels/pallas_call | solution.py:57
  89.9 1.9 %collective-permute-start.4 = (bf16[2,2,256,128]{3,2,1,0:T(8,128)(2,1)S(1)}, bf16[2,2,256,128]{3,2,1,0:T(8,128)(2,1)S(1)}, u32[]{:S(2)}, u32[]{:S(2)}) collective-permute-start(bf16[2,2,256,128]{3,2,1,0:T(8,128)(2,1)S(1)} %get-tuple-element.24), channel_id=1, source_target_pairs={{0,32},{32,0},{64,96},{96,64},{1,33},{33,1},{65,97},{97,65},{2,34}... | collective-permute-start | bytes 786440 | tf_op jit(solution)/shard_map/ppermute | solution.py:273
  91.8 4.9 %collective-permute-start.5 = (bf16[2,2,256,128]{3,2,1,0:T(8,128)(2,1)S(1)}, bf16[2,2,256,128]{3,2,1,0:T(8,128)(2,1)S(1)}, u32[]{:S(2)}, u32[]{:S(2)}) collective-permute-start(bf16[2,2,256,128]{3,2,1,0:T(8,128)(2,1)S(1)} %get-tuple-element.25), channel_id=1, source_target_pairs={{0,64},{32,96},{64,0},{96,32},{1,65},{33,97},{65,1},{97,33},{2,66}... | collective-permute-start | bytes 786440 | tf_op jit(solution)/shard_map/ppermute | solution.py:273
  96.7 4.6 %collective-permute-start.6 = (bf16[2,2,256,128]{3,2,1,0:T(8,128)(2,1)S(1)}, bf16[2,2,256,128]{3,2,1,0:T(8,128)(2,1)S(1)}, u32[]{:S(2)}, u32[]{:S(2)}) collective-permute-start(bf16[2,2,256,128]{3,2,1,0:T(8,128)(2,1)S(1)} %get-tuple-element.26), channel_id=1, source_target_pairs={{0,96},{32,64},{64,32},{96,0},{1,97},{33,65},{65,33},{97,1},{2,98}... | collective-permute-start | bytes 786440 | tf_op jit(solution)/shard_map/ppermute | solution.py:273
  101.3 16.0 %collective-permute-done.5.refs_2_ = bf16[2,2,256,128]{3,2,1,0:T(8,128)(2,1)S(1)} collective-permute-done((bf16[2,2,256,128]{3,2,1,0:T(8,128)(2,1)S(1)}, bf16[2,2,256,128]{3,2,1,0:T(8,128)(2,1)S(1)}, u32[]{:S(2)}, u32[]{:S(2)}) %collective-permute-start.5) | collective-permute-done | bytes 262176 | tf_op jit(solution)/shard_map/ppermute | solution.py:273
  117.3 4.8 %collective-permute-done.6.refs_3_ = bf16[2,2,256,128]{3,2,1,0:T(8,128)(2,1)S(1)} collective-permute-done((bf16[2,2,256,128]{3,2,1,0:T(8,128)(2,1)S(1)}, bf16[2,2,256,128]{3,2,1,0:T(8,128)(2,1)S(1)}, u32[]{:S(2)}, u32[]{:S(2)}) %collective-permute-start.6) | collective-permute-done | bytes 262176 | tf_op jit(solution)/shard_map/ppermute | solution.py:273
  122.2 4.3 %collective-permute-start.7 = (bf16[4,2,256,128]{3,2,1,0:T(8,128)(2,1)S(1)}, bf16[4,2,256,128]{3,2,1,0:T(8,128)(2,1)S(1)}, u32[]{:S(2)}, u32[]{:S(2)}) collective-permute-start(bf16[4,2,256,128]{3,2,1,0:T(8,128)(2,1)S(1)} %pad_maximum_fusion), channel_id=1, source_target_pairs={{0,1},{1,0},{2,3},{3,2},{4,5},{5,4},{6,7},{7,6},{8,9},{9,8},{10,11... | collective-permute-start | bytes 1572872 | tf_op jit(solution)/shard_map/ppermute | solution.py:274
  126.5 1.2 late_place.1.place_ref
  128.0 0.7 copy-done.4
  128.7 1.2 score_terms.1
  129.9 2.3 %collective-permute-start.8 = (f32[8,4,16,128]{3,2,1,0:T(8,128)S(1)}, f32[8,4,16,128]{3,2,1,0:T(8,128)S(1)}, u32[]{:S(2)}, u32[]{:S(2)}) collective-permute-start(f32[8,4,16,128]{3,2,1,0:T(8,128)S(1)} %get-tuple-element.28), channel_id=1, source_target_pairs={{0,1},{1,0},{2,3},{3,2},{4,5},{5,4},{6,7},{7,6},{8,9},{9,8},{10,11... | collective-permute-start | bytes 786440 | tf_op jit(solution)/shard_map/ppermute | solution.py:286
  132.2 1.1 collective-permute-done.8
  133.4 11.4 %all_to_all.37 = bf16[8,4,16,128]{3,2,1,0:T(8,128)(2,1)S(1)} all-to-all(bf16[8,4,16,128]{3,2,1,0:T(8,128)(2,1)S(1)} %add_convert_fusion), channel_id=1, replica_groups=mesh['yh'=4,'zl'=4,'zh'=2,'yl'=2,'x'=4,'c'=2] {'yl','x'}, dimensions={0} | all-to-all | bytes 262144 | tf_op jit(solution)/shard_map/all_to_all | solution.py:37
  144.8 11.4 %all_to_all.38 = f32[4,16,128]{2,1,0:T(8,128)S(1)} all-to-all(f32[4,16,128]{2,1,0:T(8,128)S(1)} %convert_reduce_fusion.1), channel_id=1, replica_groups=mesh['yh'=4,'zl'=4,'zh'=2,'yl'=2,'x'=4,'c'=2] {'zl'}, dimensions={0} | all-to-all | bytes 65536 | tf_op jit(solution)/shard_map/all_to_all | solution.py:37
  (31 shorter events, 2.6 us)
Async XLA Ops:
  5.5 11.2 %collective-permute-start = (f32[8,32,1024]{2,1,0:T(8,128)}, f32[8,32,1024]{2,1,0:T(8,128)S(1)}, u32[]{:S(2)}, u32[]{:S(2)}) collective-permute-start(f32[8,32,1024]{2,1,0:T(8,128)} %get-tuple-element.18), channel_id=1, source_target_pairs={{0,1},{1,0},{2,3},{3,2},{4,5},{5,4},{6,7},{7,6},{8,9},{9,8},{10,11... | collective-permute-start | bytes 3145736 | tf_op jit(solution)/shard_map/ppermute | solution.py:259
  16.7 12.8 %copy-start.3 = (s32[1024]{0:T(1024)S(1)}, s32[1024]{0:T(1024)}, u32[]{:S(2)}) copy-start(s32[1024]{0:T(1024)} %param.12) | copy-start | bytes 12292
  18.1 39.7 %copy-start.5 = (f32[4096]{0:T(1024)S(1)}, f32[4096]{0:T(1024)}, u32[]{:S(2)}) copy-start(f32[4096]{0:T(1024)} %param.15) | copy-start | bytes 49156
  18.1 39.8 %copy-start.2 = (s32[3]{0:T(128)S(1)}, s32[3]{0:T(128)}, u32[]{:S(2)}) copy-start(s32[3]{0:T(128)} %pad_add_fusion.place_ref) | copy-start | bytes 40
  30.2 17.2 %all-to-all-start.2 = ((bf16[8,144,128]{2,1,0:T(8,128)(2,1)}), bf16[8,144,128]{2,1,0:T(8,128)(2,1)S(1)}, u32[]{:S(2)}, u32[]{:S(2)}) async-start(bf16[8,144,128]{2,1,0:T(8,128)(2,1)} %get-tuple-element.20), calls=%async_computation.2 | async-start | bytes 589824 | tf_op jit(solution)/shard_map/all_to_all | solution.py:37
  37.3 0.7 collective-permute-start.1
  48.1 40.0 %copy-start = (s32[128,4096]{1,0:T(8,128)S(1)}, s32[128,4096]{1,0:T(8,128)}, u32[]{:S(2)}) copy-start(s32[128,4096]{1,0:T(8,128)} %codes_ref.1) | copy-start | bytes 6291460
  48.1 40.0 %copy-start.1 = (s32[4096]{0:T(1024)S(1)}, s32[4096]{0:T(1024)}, u32[]{:S(2)}) copy-start(s32[4096]{0:T(1024)} %param.14) | copy-start | bytes 49156
  48.1 13.6 %all-to-all-start.1 = ((bf16[8,16,1024]{2,1,0:T(8,128)(2,1)}), bf16[8,16,1024]{2,1,0:T(8,128)(2,1)S(1)}, u32[]{:S(2)}, u32[]{:S(2)}) async-start(bf16[8,16,1024]{2,1,0:T(8,128)(2,1)} %broadcast_in_dim.2), calls=%async_computation.1 | async-start | bytes 524288 | tf_op jit(solution)/shard_map/all_to_all | solution.py:37
  52.8 9.0 %collective-permute-start.2 = (bf16[8,144,128]{2,1,0:T(8,128)(2,1)S(1)}, bf16[8,144,128]{2,1,0:T(8,128)(2,1)S(1)}, u32[]{:S(2)}, u32[]{:S(2)}) collective-permute-start(bf16[8,144,128]{2,1,0:T(8,128)(2,1)S(1)} %all-to-all-done.2.own_ref), channel_id=1, source_target_pairs={{0,1},{1,0},{2,3},{3,2},{4,5},{5,4},{6,7},{7,6},{8,9},{9,8},{10,11... | collective-permute-start | bytes 884744 | tf_op jit(solution)/shard_map/ppermute | solution.py:269
  58.5 3.1 %collective-permute-start.3 = (f32[16,1,16]{2,1,0:T(1,128)S(1)}, f32[16,1,16]{2,1,0:T(1,128)S(1)}, u32[]{:S(2)}, u32[]{:S(2)}) collective-permute-start(f32[16,1,16]{2,1,0:T(1,128)S(1)} %get-tuple-element.22), channel_id=1, source_target_pairs={{0,1},{1,0},{2,3},{3,2},{4,5},{5,4},{6,7},{7,6},{8,9},{9,8},{10,11... | collective-permute-start | bytes 3080 | tf_op jit(solution)/shard_map/ppermute | solution.py:277
  81.2 46.8 %all-to-all-start.4 = ((bf16[8,64,512]{2,1,0:T(8,128)(2,1)}), bf16[8,64,512]{2,1,0:T(8,128)(2,1)S(1)}, u32[]{:S(2)}, u32[]{:S(2)}) async-start(bf16[8,64,512]{2,1,0:T(8,128)(2,1)} %spread_share.1), calls=%async_computation.4 | async-start | bytes 1048576 | tf_op jit(solution)/shard_map/all_to_all | solution.py:37
  89.9 11.4 %collective-permute-start.4 = (bf16[2,2,256,128]{3,2,1,0:T(8,128)(2,1)S(1)}, bf16[2,2,256,128]{3,2,1,0:T(8,128)(2,1)S(1)}, u32[]{:S(2)}, u32[]{:S(2)}) collective-permute-start(bf16[2,2,256,128]{3,2,1,0:T(8,128)(2,1)S(1)} %get-tuple-element.24), channel_id=1, source_target_pairs={{0,32},{32,0},{64,96},{96,64},{1,33},{33,1},{65,97},{97,65},{2,34}... | collective-permute-start | bytes 786440 | tf_op jit(solution)/shard_map/ppermute | solution.py:273
  91.8 25.5 %collective-permute-start.5 = (bf16[2,2,256,128]{3,2,1,0:T(8,128)(2,1)S(1)}, bf16[2,2,256,128]{3,2,1,0:T(8,128)(2,1)S(1)}, u32[]{:S(2)}, u32[]{:S(2)}) collective-permute-start(bf16[2,2,256,128]{3,2,1,0:T(8,128)(2,1)S(1)} %get-tuple-element.25), channel_id=1, source_target_pairs={{0,64},{32,96},{64,0},{96,32},{1,65},{33,97},{65,1},{97,33},{2,66}... | collective-permute-start | bytes 786440 | tf_op jit(solution)/shard_map/ppermute | solution.py:273
  96.7 25.5 %collective-permute-start.6 = (bf16[2,2,256,128]{3,2,1,0:T(8,128)(2,1)S(1)}, bf16[2,2,256,128]{3,2,1,0:T(8,128)(2,1)S(1)}, u32[]{:S(2)}, u32[]{:S(2)}) collective-permute-start(bf16[2,2,256,128]{3,2,1,0:T(8,128)(2,1)S(1)} %get-tuple-element.26), channel_id=1, source_target_pairs={{0,96},{32,64},{64,32},{96,0},{1,97},{33,65},{65,33},{97,1},{2,98}... | collective-permute-start | bytes 786440 | tf_op jit(solution)/shard_map/ppermute | solution.py:273
  122.2 5.8 %collective-permute-start.7 = (bf16[4,2,256,128]{3,2,1,0:T(8,128)(2,1)S(1)}, bf16[4,2,256,128]{3,2,1,0:T(8,128)(2,1)S(1)}, u32[]{:S(2)}, u32[]{:S(2)}) collective-permute-start(bf16[4,2,256,128]{3,2,1,0:T(8,128)(2,1)S(1)} %pad_maximum_fusion), channel_id=1, source_target_pairs={{0,1},{1,0},{2,3},{3,2},{4,5},{5,4},{6,7},{7,6},{8,9},{9,8},{10,11... | collective-permute-start | bytes 1572872 | tf_op jit(solution)/shard_map/ppermute | solution.py:274
  128.0 0.7 copy-start.4
  129.9 3.4 %collective-permute-start.8 = (f32[8,4,16,128]{3,2,1,0:T(8,128)S(1)}, f32[8,4,16,128]{3,2,1,0:T(8,128)S(1)}, u32[]{:S(2)}, u32[]{:S(2)}) collective-permute-start(f32[8,4,16,128]{3,2,1,0:T(8,128)S(1)} %get-tuple-element.28), channel_id=1, source_target_pairs={{0,1},{1,0},{2,3},{3,2},{4,5},{5,4},{6,7},{7,6},{8,9},{9,8},{10,11... | collective-permute-start | bytes 786440 | tf_op jit(solution)/shard_map/ppermute | solution.py:286
